TPU v7x, 32 devices: a whole 2x2x4 slice. The times are simulated.
32 devices in a mesh: gr: 8 (over z, core), gc: 4 (over y, x).
Axes of the slice: x: 2, y: 2, z: 4, core: 2. Of those that a mesh axis runs over, the one named last changes fastest.
Arguments:
- projectors: bfloat16 [2, 8192, 9216], P(None, ('gr', 'gc')), may hold values from -0.0625 to 0.0625
- wavefunctions: bfloat16 [2, 8192, 512], P(None, ('gr', 'gc')), may hold values from -6 to 6
- coupling: float32 [512, 18, 18], P('gc'), may hold values from -1.5 to 1.5
- atom_order: int32 [512], replicated, may hold values from 0 to 511, each once
Outputs:
- coupled: float32 [9216, 512], P('gc', 'gr')
Inputs may be any that keep to these rules, and one draw needn't show every extreme that they name: `atom_order`: a permutation of the atoms.
All inputs are finite; a program needn't handle non-finite values.
Results may differ from a plain program's by a relative error of at most 0.0003.
Values sent between devices are 32-bit elements; how exact they have to be, the bound alone decides.
No kernel may reach another device: no remote copies, remote signals or barrier semaphores. Data moves between devices by JAX's collectives and lax.ppermute only.
A program may use at most 128 MiB of HBM per device.

v0:
```python
import functools

import jax
import jax.numpy as jnp
from jax import lax
from jax.experimental import pallas as pl
from jax.experimental.pallas import tpu as pltpu
from jax.sharding import PartitionSpec as P


PLAN = ((1, 1), (2, 2, 1, 1))
UNITS = 8
GROUP = 4
PAD = 8
LANES = 128


def project_body(atoms_ref, me_ref, proj_ref, waves_ref, *rest, steps, owners, nh, per_block, width, offsets, sizes, local_atoms):
    outs, nat_ref = rest[:-1], rest[-1]
    step = pl.program_id(0)
    block = proj_ref.shape[1]

    @pl.when(step < steps)
    def _():
        start = pl.multiple_of(PAD + step * block, 8)
        term = lax.dot_general(
            proj_ref[...], waves_ref[...], (((0,), (0,)), ((), ())), preferred_element_type=jnp.float32
        )
        for lane in range(term.shape[1] // LANES):
            nat_ref[lane, pl.ds(start, block), :] = term[:, lane * LANES:(lane + 1) * LANES]

    tiles = GROUP * nh // 8
    for chunk, (offset, size) in enumerate(zip(offsets, sizes)):
        keep_ref, send_ref = outs[2 * chunk], outs[2 * chunk + 1]
        first = steps + owners * sum(sizes[:chunk])

        @pl.when((step >= first) & (step < first + owners * size))
        def _():
            owner = me_ref[0] ^ ((step - first) // size)
            base = owner * local_atoms + (offset + (step - first) % size) * per_block

            @pl.loop(0, per_block // GROUP)
            def _(g):
                slot = base + g * GROUP
                starts = [atoms_ref[slot + t] * nh + PAD for t in range(GROUP)]
                for tile in range(tiles):
                    row = tile * 8
                    a = row // nh
                    at = pl.multiple_of(g * (GROUP * nh) + row, 8)
                    for lane in range(2 * width // LANES):
                        vals = nat_ref[lane, pl.ds(starts[a] + (row - a * nh), 8), :]
                        if (row + 7) // nh != a:
                            cut = (a + 1) * nh - row
                            nxt = nat_ref[lane, pl.ds(starts[a + 1] - cut, 8), :]
                            sub = lax.broadcasted_iota(jnp.int32, vals.shape, 0)
                            vals = jnp.where(sub < cut, vals, nxt)
                        out_ref = keep_ref if lane * LANES < width else send_ref
                        out_ref[pl.ds(at, 8), pl.ds(lane * LANES % width, LANES)] = vals


def project(columns, waves, atoms, me, owners, nh, per_block, offset, sizes):
    k, nkb = columns.shape
    bands = waves.shape[1]
    width = bands // 2
    block = nkb // 8
    steps = nkb // block
    rows = per_block * nh

    def out_map(first, count):
        return lambda i, *_: (jnp.clip(i - first, 0, count - 1), 0)

    specs, shapes, offsets = [], [], []
    for chunk, size in enumerate(sizes):
        offsets.append(offset + sum(sizes[:chunk]))
        for _ in range(2):
            specs.append(pl.BlockSpec((rows, width), out_map(steps + owners * sum(sizes[:chunk]), owners * size)))
            shapes.append(jax.ShapeDtypeStruct((owners * size * rows, width), jnp.float32))
    body = functools.partial(
        project_body, steps=steps, owners=owners, nh=nh, per_block=per_block, width=width,
        offsets=offsets, sizes=sizes, local_atoms=atoms.shape[0] // owners,
    )
    return pl.pallas_call(
        body,
        grid_spec=pltpu.PrefetchScalarGridSpec(
            num_scalar_prefetch=2,
            grid=(steps + owners * sum(sizes),),
            in_specs=[
                pl.BlockSpec((k, block), lambda i, *_: (0, jnp.minimum(i, steps - 1))),
                pl.BlockSpec((k, bands), lambda i, *_: (0, 0)),
            ],
            out_specs=specs,
            scratch_shapes=[pltpu.VMEM((bands // LANES, nkb + 2 * PAD, LANES), jnp.float32)],
        ),
        out_shape=shapes,
        compiler_params=pltpu.CompilerParams(
            dimension_semantics=("arbitrary",), vmem_limit_bytes=48 * 1024 * 1024
        ),
        cost_estimate=pl.CostEstimate(
            flops=2 * k * nkb * bands, transcendentals=0, bytes_accessed=2 * k * nkb + 4 * nkb * bands
        ),
    )(atoms, me, columns, waves)


def swap(x, axis, bit):
    n = lax.axis_size(axis)
    return lax.ppermute(x, axis, [(i, i ^ bit) for i in range(n)])


def bits_of(n):
    return [1 << b for b in range(n.bit_length() - 1)]


def shards(projectors, wavefunctions, coupling, atom_order):
    k = 2 * projectors.shape[1]
    nkb = projectors.shape[2]
    bands = wavefunctions.shape[2]
    atoms = atom_order.shape[0]
    nh = nkb // atoms
    gr, gc = lax.axis_size("gr"), lax.axis_size("gc")
    nz, own = gr // 2, bands // gr
    local_atoms = coupling.shape[0]
    per_block = local_atoms // UNITS
    me_r, me_c = lax.axis_index("gr"), lax.axis_index("gc")

    j = jnp.arange(bands, dtype=jnp.int32)
    rel_core, rel = j // (nz * own), (j // own) % nz
    rel_z = jnp.zeros_like(rel)
    for n, bit in enumerate(bits_of(nz)):
        rel_z = rel_z + bit * ((rel // (nz >> (n + 1))) % 2)
    source = (me_r ^ (2 * rel_z + rel_core)) * own + j % own
    spread = jnp.where(jnp.arange(bands, dtype=jnp.int32)[:, None] == source[None, :], 2.0, 0.0).astype(jnp.bfloat16)
    waves = jnp.dot(
        wavefunctions.reshape(k, bands), spread, preferred_element_type=jnp.float32
    ).astype(jnp.bfloat16)

    columns = projectors.reshape(k, nkb)
    me = me_c.astype(jnp.int32).reshape(1)
    sums, spans, offset = [], [], 0
    for sizes in PLAN:
        outs = list(project(columns, waves, atom_order, me, gc, nh, per_block, offset, sizes))
        if offset > 0:
            coupling, outs[-2] = lax.optimization_barrier((coupling, outs[-2]))
        for c, size in enumerate(sizes):
            spans.append((offset * per_block * nh, size * per_block))
            offset += size
            sums.append(outs[2 * c] + swap(outs[2 * c + 1], "gr", 1))
        if offset < UNITS:
            me, sums[-1] = lax.optimization_barrier((me, sums[-1]))

    per_group = min(8, per_block)
    side = per_group * nh
    at = jnp.arange(side, dtype=jnp.int32)
    repeat = (jnp.arange(nh, dtype=jnp.int32)[:, None] == (at % nh)[None, :]).astype(jnp.float32)
    wide = jnp.dot(coupling.reshape(local_atoms * nh, nh), repeat, precision=lax.Precision.HIGHEST)
    atom_of = (jnp.arange(local_atoms * nh, dtype=jnp.int32) // nh) % per_group
    blocks = jnp.where(atom_of[:, None] == (at // nh)[None, :], wide, 0.0)

    pieces = []
    for c, (s, (start, count)) in enumerate(zip(sums, spans)):
        rows = count * nh
        bits = bits_of(gc)
        s = s.reshape([2] * len(bits) + [rows, s.shape[1]])
        left = bits[::-1]
        for bit in bits if c % 2 == 0 else bits[::-1]:
            axis = left.index(bit)
            left = left[:axis] + left[axis + 1:]
            mine = lax.index_in_dim(s, 0, axis, keepdims=False)
            other = lax.index_in_dim(s, 1, axis, keepdims=False)
            s = mine + swap(other, "gc", bit)
        for bit in bits_of(nz):
            half = s.shape[1] // 2
            fold = max(1, LANES // half)
            other = s[:, half:]
            if fold > 1:
                other = jnp.concatenate(jnp.split(other, fold, axis=0), axis=1)
            got = swap(other, "gr", 2 * bit)
            if fold > 1:
                got = jnp.concatenate(jnp.split(got, fold, axis=1), axis=0)
            s = s[:, :half] + got
        done = lax.dot_general(
            blocks[start:start + rows].reshape(count // per_group, side, side),
            s.reshape(count // per_group, side, s.shape[1]), (((2,), (1,)), ((0,), (0,))),
            precision=lax.Precision.HIGHEST, preferred_element_type=jnp.float32,
        )
        pieces.append(done.reshape(rows, s.shape[1]))
    return jnp.concatenate(pieces, axis=0)


def solution(mesh):
    return jax.shard_map(
        shards,
        mesh=mesh,
        in_specs=(
            P(None, ("gr", "gc"), None),
            P(None, ("gr", "gc"), None),
            P("gc", None, None),
            P(),
        ),
        out_specs=P("gc", "gr"),
        check_vma=False,
    )
```

profile of v0, /device:TPU:0, one launch (start us, length us, event | category | flops | bytes accessed | tf_op | source)
XLA Modules:
  0.0 186.6 jit_solution(16259527148471158986)
XLA Ops:
  1.5 11.1 %shard_map.46 = (f32[1152,256]{1,0:T(8,128)S(1)}, f32[1152,256]{1,0:T(8,128)S(1)}, f32[1152,256]{1,0:T(8,128)S(1)}, f32[1152,256]{1,0:T(8,128)S(1)}) custom-call(s32[512]{0:T(512)S(1)} %copy-done.3, s32[1]{0:T(128)} %bitcast.me_ref, bf16[512,9216]{1,0:T(8,128)(2,1)} %bitcast.144, bf16[512,512]{1,0:T(8,128)(2,1)S(1)} %fusion.waves_ref), custom_call_target="tpu_custom_call" | custom-call | flops 4831838208 | bytes 28311552 | tf_op jit(solution)/shard_map/pallas_call | solution.py:82
  16.9 2.9 %collective-permute-start.6 = (f32[2,288,256]{2,1,0:T(8,128)}, f32[2,288,256]{2,1,0:T(8,128)}, u32[]{:S(2)}, u32[]{:S(2)}) collective-permute-start(f32[2,288,256]{2,1,0:T(8,128)} %bitcast.13), channel_id=1, source_target_pairs={{0,2},{1,3},{2,0},{3,1},{4,6},{5,7},{6,4},{7,5},{8,10},{9,11},{10,... | collective-permute-start | bytes 1769480 | tf_op jit(solution)/shard_map/ppermute | solution.py:106
  22.4 20.3 %shard_map.47 = (f32[2304,256]{1,0:T(8,128)}, f32[2304,256]{1,0:T(8,128)}, f32[2304,256]{1,0:T(8,128)}, f32[2304,256]{1,0:T(8,128)}, f32[1152,256]{1,0:T(8,128)S...) custom-call(s32[512]{0:T(512)S(1)} %copy-done.3, s32[1]{0:T(128)} %bitcast.me_ref, ...), custom_call_target="tpu_custom_call" | custom-call | flops 4831838208 | bytes 28311552 | tf_op jit(solution)/shard_map/pallas_call | solution.py:82
  43.7 2.4 %copy.48 = f32[128,18,18]{1,0,2:T(8,128)} copy(f32[128,18,18]{0,2,1:T(8,128)} %param.6) | data formatting | bytes 331776 | tf_op jit(solution)/shard_map/optimization_barrier | solution.py:142
  46.1 2.6 %reshape.219 = f32[2304,18]{0,1:T(8,128)} reshape(f32[128,18,18]{1,0,2:T(8,128)} %copy.48) | data formatting | bytes 331776 | tf_op jit(solution)/shard_map/reshape | solution.py:154
  59.3 2.1 %copy.89 = f32[576,144]{1,0:T(8,128)} copy(f32[576,144]{0,1:T(8,128)} %get-tuple-element.43) | data formatting | bytes 663552 | tf_op jit(solution)/shard_map/reshape | solution.py:181
  66.7 2.0 %copy.86 = f32[576,144]{1,0:T(8,128)} copy(f32[576,144]{0,1:T(8,128)} %get-tuple-element.44) | data formatting | bytes 663552 | tf_op jit(solution)/shard_map/reshape | solution.py:181
  73.7 3.0 %collective-permute-done.8 = f32[288,128]{1,0:T(8,128)S(1)} collective-permute-done((f32[288,128]{1,0:T(8,128)S(1)}, f32[288,128]{1,0:T(8,128)S(1)}, u32[]{:S(2)}, u32[]{:S(2)}) %collective-permute-start.8) | collective-permute-done | bytes 147488 | tf_op jit(solution)/shard_map/ppermute | solution.py:106
  78.7 3.2 %collective-permute-done.4 = f32[288,128]{1,0:T(8,128)S(1)} collective-permute-done((f32[288,128]{1,0:T(8,128)S(1)}, f32[288,128]{1,0:T(8,128)S(1)}, u32[]{:S(2)}, u32[]{:S(2)}) %collective-permute-start.4) | collective-permute-done | bytes 147488 | tf_op jit(solution)/shard_map/ppermute | solution.py:106
  81.9 2.7 %collective-permute-start.9 = (f32[144,128]{1,0:T(8,128)S(1)}, f32[144,128]{1,0:T(8,128)S(1)}, u32[]{:S(2)}, u32[]{:S(2)}) collective-permute-start(f32[144,128]{1,0:T(8,128)S(1)} %pad_maximum_fusion.3), channel_id=1, source_target_pairs={{0,16},{4,20},{8,24},{12,28},{16,0},{20,4},{24,8},{28,12},{1,17},{... | collective-permute-start | bytes 221192 | tf_op jit(solution)/shard_map/ppermute | solution.py:106
  84.8 2.3 %collective-permute-done.9 = f32[144,128]{1,0:T(8,128)S(1)} collective-permute-done((f32[144,128]{1,0:T(8,128)S(1)}, f32[144,128]{1,0:T(8,128)S(1)}, u32[]{:S(2)}, u32[]{:S(2)}) %collective-permute-start.9) | collective-permute-done | bytes 73760 | tf_op jit(solution)/shard_map/ppermute | solution.py:106
  87.1 2.8 %collective-permute-start.5 = (f32[144,128]{1,0:T(8,128)S(1)}, f32[144,128]{1,0:T(8,128)S(1)}, u32[]{:S(2)}, u32[]{:S(2)}) collective-permute-start(f32[144,128]{1,0:T(8,128)S(1)} %pad_maximum_fusion.2), channel_id=1, source_target_pairs={{0,16},{4,20},{8,24},{12,28},{16,0},{20,4},{24,8},{28,12},{1,17},{... | collective-permute-start | bytes 221192 | tf_op jit(solution)/shard_map/ppermute | solution.py:106
  94.5 8.2 %collective-permute-done.21 = f32[2,288,256]{2,1,0:T(8,128)S(1)} collective-permute-done((f32[2,288,256]{2,1,0:T(8,128)S(1)}, f32[2,288,256]{2,1,0:T(8,128)S(1)}, u32[]{:S(2)}, u32[]{:S(2)}) %collective-permute-start.21) | collective-permute-done | bytes 589856 | tf_op jit(solution)/shard_map/ppermute | solution.py:106
  104.4 3.3 %collective-permute-done.26 = f32[2,288,256]{2,1,0:T(8,128)S(1)} collective-permute-done((f32[2,288,256]{2,1,0:T(8,128)S(1)}, f32[2,288,256]{2,1,0:T(8,128)S(1)}, u32[]{:S(2)}, u32[]{:S(2)}) %collective-permute-start.26) | collective-permute-done | bytes 589856 | tf_op jit(solution)/shard_map/ppermute | solution.py:106
  110.9 2.2 %collective-permute-start.23 = (f32[288,128]{1,0:T(8,128)S(1)}, f32[288,128]{1,0:T(8,128)S(1)}, u32[]{:S(2)}, u32[]{:S(2)}) collective-permute-start(f32[288,128]{1,0:T(8,128)S(1)} %slice.252), channel_id=1, source_target_pairs={{0,8},{4,12},{8,0},{12,4},{16,24},{20,28},{24,16},{28,20},{1,9},{5... | collective-permute-start | bytes 442376 | tf_op jit(solution)/shard_map/ppermute | solution.py:106
  114.7 2.0 %collective-permute-start.28 = (f32[288,128]{1,0:T(8,128)S(1)}, f32[288,128]{1,0:T(8,128)S(1)}, u32[]{:S(2)}, u32[]{:S(2)}) collective-permute-start(f32[288,128]{1,0:T(8,128)S(1)} %slice.260), channel_id=1, source_target_pairs={{0,8},{4,12},{8,0},{12,4},{16,24},{20,28},{24,16},{28,20},{1,9},{5... | collective-permute-start | bytes 442376 | tf_op jit(solution)/shard_map/ppermute | solution.py:106
  117.0 3.2 %collective-permute-start.24 = (f32[144,128]{1,0:T(8,128)S(1)}, f32[144,128]{1,0:T(8,128)S(1)}, u32[]{:S(2)}, u32[]{:S(2)}) collective-permute-start(f32[144,128]{1,0:T(8,128)S(1)} %pad_maximum_fusion.4), channel_id=1, source_target_pairs={{0,16},{4,20},{8,24},{12,28},{16,0},{20,4},{24,8},{28,12},{1,17},{... | collective-permute-start | bytes 221192 | tf_op jit(solution)/shard_map/ppermute | solution.py:106
  120.5 2.3 %collective-permute-start.29 = (f32[144,128]{1,0:T(8,128)S(1)}, f32[144,128]{1,0:T(8,128)S(1)}, u32[]{:S(2)}, u32[]{:S(2)}) collective-permute-start(f32[144,128]{1,0:T(8,128)S(1)} %pad_maximum_fusion.5), channel_id=1, source_target_pairs={{0,16},{4,20},{8,24},{12,28},{16,0},{20,4},{24,8},{28,12},{1,17},{... | collective-permute-start | bytes 221192 | tf_op jit(solution)/shard_map/ppermute | solution.py:106
  126.5 2.0 %add.216 = f32[2304,256]{1,0:T(8,128)S(1)} add(f32[2304,256]{1,0:T(8,128)S(1)} %copy-done.6, f32[2304,256]{1,0:T(8,128)} %collective-permute-done.15) | non-fusion elementwise | flops 589824 | bytes 7077888 | tf_op jit(solution)/shard_map/add | solution.py:146
  130.8 16.3 %collective-permute-done.11 = f32[2,576,256]{2,1,0:T(8,128)S(1)} collective-permute-done((f32[2,576,256]{2,1,0:T(8,128)S(1)}, f32[2,576,256]{2,1,0:T(8,128)S(1)}, u32[]{:S(2)}, u32[]{:S(2)}) %collective-permute-start.11) | collective-permute-done | bytes 1179680 | tf_op jit(solution)/shard_map/ppermute | solution.py:106
  149.0 6.0 %collective-permute-done.16 = f32[2,576,256]{2,1,0:T(8,128)S(1)} collective-permute-done((f32[2,576,256]{2,1,0:T(8,128)S(1)}, f32[2,576,256]{2,1,0:T(8,128)S(1)}, u32[]{:S(2)}, u32[]{:S(2)}) %collective-permute-start.16) | collective-permute-done | bytes 1179680 | tf_op jit(solution)/shard_map/ppermute | solution.py:106
  156.8 4.5 %collective-permute-done.12 = f32[576,256]{1,0:T(8,128)S(1)} collective-permute-done((f32[576,256]{1,0:T(8,128)S(1)}, f32[576,256]{1,0:T(8,128)S(1)}, u32[]{:S(2)}, u32[]{:S(2)}) %collective-permute-start.12) | collective-permute-done | bytes 589856 | tf_op jit(solution)/shard_map/ppermute | solution.py:106
  166.3 5.8 %collective-permute-done.13 = f32[576,128]{1,0:T(8,128)} collective-permute-done((f32[576,128]{1,0:T(8,128)}, f32[576,128]{1,0:T(8,128)}, u32[]{:S(2)}, u32[]{:S(2)}) %collective-permute-start.13) | collective-permute-done | bytes 294944 | tf_op jit(solution)/shard_map/ppermute | solution.py:106
  176.8 5.5 %collective-permute-done.14 = f32[288,128]{1,0:T(8,128)S(1)} collective-permute-done((f32[288,128]{1,0:T(8,128)S(1)}, f32[288,128]{1,0:T(8,128)S(1)}, u32[]{:S(2)}, u32[]{:S(2)}) %collective-permute-start.14) | collective-permute-done | bytes 147488 | tf_op jit(solution)/shard_map/ppermute | solution.py:106
  (176 shorter events, 67.4 us)
Async XLA Ops:
  13.1 6.7 %collective-permute-start.1 = (f32[1152,256]{1,0:T(8,128)S(1)}, f32[1152,256]{1,0:T(8,128)S(1)}, u32[]{:S(2)}, u32[]{:S(2)}) collective-permute-start(f32[1152,256]{1,0:T(8,128)S(1)} %get-tuple-element.27), channel_id=1, source_target_pairs={{0,4},{4,0},{8,12},{12,8},{16,20},{20,16},{24,28},{28,24},{1,5},{5... | collective-permute-start | bytes 3538952 | tf_op jit(solution)/shard_map/ppermute | solution.py:106
  16.9 34.6 %collective-permute-start.6 = (f32[2,288,256]{2,1,0:T(8,128)}, f32[2,288,256]{2,1,0:T(8,128)}, u32[]{:S(2)}, u32[]{:S(2)}) collective-permute-start(f32[2,288,256]{2,1,0:T(8,128)} %bitcast.13), channel_id=1, source_target_pairs={{0,2},{1,3},{2,0},{3,1},{4,6},{5,7},{6,4},{7,5},{8,10},{9,11},{10,... | collective-permute-start | bytes 1769480 | tf_op jit(solution)/shard_map/ppermute | solution.py:106
  20.9 33.1 %collective-permute-start.2 = (f32[2,288,256]{2,1,0:T(8,128)}, f32[2,288,256]{2,1,0:T(8,128)}, u32[]{:S(2)}, u32[]{:S(2)}) collective-permute-start(f32[2,288,256]{2,1,0:T(8,128)} %slice_bitcast_fusion.8), channel_id=1, source_target_pairs={{0,1},{1,0},{2,3},{3,2},{4,5},{5,4},{6,7},{7,6},{8,9},{9,8},{10,11... | collective-permute-start | bytes 1769480 | tf_op jit(solution)/shard_map/ppermute | solution.py:106
  53.5 15.8 %collective-permute-start.7 = (f32[288,256]{1,0:T(8,128)}, f32[288,256]{1,0:T(8,128)}, u32[]{:S(2)}, u32[]{:S(2)}) collective-permute-start(f32[288,256]{1,0:T(8,128)} %slice_bitcast_fusion.14), channel_id=1, source_target_pairs={{0,1},{1,0},{2,3},{3,2},{4,5},{5,4},{6,7},{7,6},{8,9},{9,8},{10,11... | collective-permute-start | bytes 884744 | tf_op jit(solution)/shard_map/ppermute | solution.py:106
  56.0 14.9 %collective-permute-start.3 = (f32[288,256]{1,0:T(8,128)}, f32[288,256]{1,0:T(8,128)}, u32[]{:S(2)}, u32[]{:S(2)}) collective-permute-start(f32[288,256]{1,0:T(8,128)} %slice_bitcast_fusion.16), channel_id=1, source_target_pairs={{0,2},{1,3},{2,0},{3,1},{4,6},{5,7},{6,4},{7,5},{8,10},{9,11},{10,... | collective-permute-start | bytes 884744 | tf_op jit(solution)/shard_map/ppermute | solution.py:106
  68.8 21.8 %collective-permute-start.20 = (f32[1152,256]{1,0:T(8,128)}, f32[1152,256]{1,0:T(8,128)S(1)}, u32[]{:S(2)}, u32[]{:S(2)}) collective-permute-start(f32[1152,256]{1,0:T(8,128)} %copy-done.2), channel_id=1, source_target_pairs={{0,4},{4,0},{8,12},{12,8},{16,20},{20,16},{24,28},{28,24},{1,5},{5... | collective-permute-start | bytes 3538952 | tf_op jit(solution)/shard_map/ppermute | solution.py:106
  68.8 23.7 %collective-permute-start.25 = (f32[1152,256]{1,0:T(8,128)S(1)}, f32[1152,256]{1,0:T(8,128)S(1)}, u32[]{:S(2)}, u32[]{:S(2)}) collective-permute-start(f32[1152,256]{1,0:T(8,128)S(1)} %get-tuple-element.36), channel_id=1, source_target_pairs={{0,4},{4,0},{8,12},{12,8},{16,20},{20,16},{24,28},{28,24},{1,5},{5... | collective-permute-start | bytes 3538952 | tf_op jit(solution)/shard_map/ppermute | solution.py:106
  69.3 53.5 %collective-permute-start.10 = (f32[2304,256]{1,0:T(8,128)}, f32[2304,256]{1,0:T(8,128)}, u32[]{:S(2)}, u32[]{:S(2)}) collective-permute-start(f32[2304,256]{1,0:T(8,128)} %get-tuple-element.30), channel_id=1, source_target_pairs={{0,4},{4,0},{8,12},{12,8},{16,20},{20,16},{24,28},{28,24},{1,5},{5... | collective-permute-start | bytes 7077896 | tf_op jit(solution)/shard_map/ppermute | solution.py:106
  69.3 57.2 %collective-permute-start.15 = (f32[2304,256]{1,0:T(8,128)}, f32[2304,256]{1,0:T(8,128)}, u32[]{:S(2)}, u32[]{:S(2)}) collective-permute-start(f32[2304,256]{1,0:T(8,128)} %get-tuple-element.32), channel_id=1, source_target_pairs={{0,4},{4,0},{8,12},{12,8},{16,20},{20,16},{24,28},{28,24},{1,5},{5... | collective-permute-start | bytes 7077896 | tf_op jit(solution)/shard_map/ppermute | solution.py:106
  90.8 11.9 %collective-permute-start.21 = (f32[2,288,256]{2,1,0:T(8,128)S(1)}, f32[2,288,256]{2,1,0:T(8,128)S(1)}, u32[]{:S(2)}, u32[]{:S(2)}) collective-permute-start(f32[2,288,256]{2,1,0:T(8,128)S(1)} %slice_bitcast_fusion.2), channel_id=1, source_target_pairs={{0,1},{1,0},{2,3},{3,2},{4,5},{5,4},{6,7},{7,6},{8,9},{9,8},{10,11... | collective-permute-start | bytes 1769480 | tf_op jit(solution)/shard_map/ppermute | solution.py:106
  92.7 15.0 %collective-permute-start.26 = (f32[2,288,256]{2,1,0:T(8,128)S(1)}, f32[2,288,256]{2,1,0:T(8,128)S(1)}, u32[]{:S(2)}, u32[]{:S(2)}) collective-permute-start(f32[2,288,256]{2,1,0:T(8,128)S(1)} %bitcast.143), channel_id=1, source_target_pairs={{0,2},{1,3},{2,0},{3,1},{4,6},{5,7},{6,4},{7,5},{8,10},{9,11},{10,... | collective-permute-start | bytes 1769480 | tf_op jit(solution)/shard_map/ppermute | solution.py:106
  102.8 8.1 %collective-permute-start.22 = (f32[288,256]{1,0:T(8,128)S(1)}, f32[288,256]{1,0:T(8,128)S(1)}, u32[]{:S(2)}, u32[]{:S(2)}) collective-permute-start(f32[288,256]{1,0:T(8,128)S(1)} %slice_bitcast_fusion.12), channel_id=1, source_target_pairs={{0,2},{1,3},{2,0},{3,1},{4,6},{5,7},{6,4},{7,5},{8,10},{9,11},{10,... | collective-permute-start | bytes 884744 | tf_op jit(solution)/shard_map/ppermute | solution.py:106
  107.8 6.8 %collective-permute-start.27 = (f32[288,256]{1,0:T(8,128)S(1)}, f32[288,256]{1,0:T(8,128)S(1)}, u32[]{:S(2)}, u32[]{:S(2)}) collective-permute-start(f32[288,256]{1,0:T(8,128)S(1)} %slice_bitcast_fusion.10), channel_id=1, source_target_pairs={{0,1},{1,0},{2,3},{3,2},{4,5},{5,4},{6,7},{7,6},{8,9},{9,8},{10,11... | collective-permute-start | bytes 884744 | tf_op jit(solution)/shard_map/ppermute | solution.py:106
  110.9 5.9 %collective-permute-start.23 = (f32[288,128]{1,0:T(8,128)S(1)}, f32[288,128]{1,0:T(8,128)S(1)}, u32[]{:S(2)}, u32[]{:S(2)}) collective-permute-start(f32[288,128]{1,0:T(8,128)S(1)} %slice.252), channel_id=1, source_target_pairs={{0,8},{4,12},{8,0},{12,4},{16,24},{20,28},{24,16},{28,20},{1,9},{5... | collective-permute-start | bytes 442376 | tf_op jit(solution)/shard_map/ppermute | solution.py:106
  117.0 9.4 %collective-permute-start.24 = (f32[144,128]{1,0:T(8,128)S(1)}, f32[144,128]{1,0:T(8,128)S(1)}, u32[]{:S(2)}, u32[]{:S(2)}) collective-permute-start(f32[144,128]{1,0:T(8,128)S(1)} %pad_maximum_fusion.4), channel_id=1, source_target_pairs={{0,16},{4,20},{8,24},{12,28},{16,0},{20,4},{24,8},{28,12},{1,17},{... | collective-permute-start | bytes 221192 | tf_op jit(solution)/shard_map/ppermute | solution.py:106
  120.5 28.5 %collective-permute-start.29 = (f32[144,128]{1,0:T(8,128)S(1)}, f32[144,128]{1,0:T(8,128)S(1)}, u32[]{:S(2)}, u32[]{:S(2)}) collective-permute-start(f32[144,128]{1,0:T(8,128)S(1)} %pad_maximum_fusion.5), channel_id=1, source_target_pairs={{0,16},{4,20},{8,24},{12,28},{16,0},{20,4},{24,8},{28,12},{1,17},{... | collective-permute-start | bytes 221192 | tf_op jit(solution)/shard_map/ppermute | solution.py:106
  124.8 22.3 %collective-permute-start.11 = (f32[2,576,256]{2,1,0:T(8,128)S(1)}, f32[2,576,256]{2,1,0:T(8,128)S(1)}, u32[]{:S(2)}, u32[]{:S(2)}) collective-permute-start(f32[2,576,256]{2,1,0:T(8,128)S(1)} %slice_bitcast_fusion), channel_id=1, source_target_pairs={{0,1},{1,0},{2,3},{3,2},{4,5},{5,4},{6,7},{7,6},{8,9},{9,8},{10,11... | collective-permute-start | bytes 3538952 | tf_op jit(solution)/shard_map/ppermute | solution.py:106
  128.6 26.4 %collective-permute-start.16 = (f32[2,576,256]{2,1,0:T(8,128)S(1)}, f32[2,576,256]{2,1,0:T(8,128)S(1)}, u32[]{:S(2)}, u32[]{:S(2)}) collective-permute-start(f32[2,576,256]{2,1,0:T(8,128)S(1)} %bitcast.138), channel_id=1, source_target_pairs={{0,2},{1,3},{2,0},{3,1},{4,6},{5,7},{6,4},{7,5},{8,10},{9,11},{10,... | collective-permute-start | bytes 3538952 | tf_op jit(solution)/shard_map/ppermute | solution.py:106
  147.3 14.0 %collective-permute-start.12 = (f32[576,256]{1,0:T(8,128)S(1)}, f32[576,256]{1,0:T(8,128)S(1)}, u32[]{:S(2)}, u32[]{:S(2)}) collective-permute-start(f32[576,256]{1,0:T(8,128)S(1)} %slice_bitcast_fusion.6), channel_id=1, source_target_pairs={{0,2},{1,3},{2,0},{3,1},{4,6},{5,7},{6,4},{7,5},{8,10},{9,11},{10,... | collective-permute-start | bytes 1769480 | tf_op jit(solution)/shard_map/ppermute | solution.py:106
  155.2 9.9 %collective-permute-start.17 = (f32[576,256]{1,0:T(8,128)S(1)}, f32[576,256]{1,0:T(8,128)S(1)}, u32[]{:S(2)}, u32[]{:S(2)}) collective-permute-start(f32[576,256]{1,0:T(8,128)S(1)} %slice_bitcast_fusion.4), channel_id=1, source_target_pairs={{0,1},{1,0},{2,3},{3,2},{4,5},{5,4},{6,7},{7,6},{8,9},{9,8},{10,11... | collective-permute-start | bytes 1769480 | tf_op jit(solution)/shard_map/ppermute | solution.py:106
  162.1 10.0 %collective-permute-start.13 = (f32[576,128]{1,0:T(8,128)}, f32[576,128]{1,0:T(8,128)}, u32[]{:S(2)}, u32[]{:S(2)}) collective-permute-start(f32[576,128]{1,0:T(8,128)} %slice.236), channel_id=1, source_target_pairs={{0,8},{4,12},{8,0},{12,4},{16,24},{20,28},{24,16},{28,20},{1,9},{5... | collective-permute-start | bytes 884744 | tf_op jit(solution)/shard_map/ppermute | solution.py:106
  165.2 9.9 %collective-permute-start.18 = (f32[576,128]{1,0:T(8,128)S(1)}, f32[576,128]{1,0:T(8,128)S(1)}, u32[]{:S(2)}, u32[]{:S(2)}) collective-permute-start(f32[576,128]{1,0:T(8,128)S(1)} %slice.244), channel_id=1, source_target_pairs={{0,8},{4,12},{8,0},{12,4},{16,24},{20,28},{24,16},{28,20},{1,9},{5... | collective-permute-start | bytes 884744 | tf_op jit(solution)/shard_map/ppermute | solution.py:106
  173.4 8.8 %collective-permute-start.14 = (f32[288,128]{1,0:T(8,128)S(1)}, f32[288,128]{1,0:T(8,128)S(1)}, u32[]{:S(2)}, u32[]{:S(2)}) collective-permute-start(f32[288,128]{1,0:T(8,128)S(1)} %pad_maximum_fusion), channel_id=1, source_target_pairs={{0,16},{4,20},{8,24},{12,28},{16,0},{20,4},{24,8},{28,12},{1,17},{... | collective-permute-start | bytes 442376 | tf_op jit(solution)/shard_map/ppermute | solution.py:106
  175.5 8.3 %collective-permute-start.19 = (f32[288,128]{1,0:T(8,128)S(1)}, f32[288,128]{1,0:T(8,128)S(1)}, u32[]{:S(2)}, u32[]{:S(2)}) collective-permute-start(f32[288,128]{1,0:T(8,128)S(1)} %pad_maximum_fusion.1), channel_id=1, source_target_pairs={{0,16},{4,20},{8,24},{12,28},{16,0},{20,4},{24,8},{28,12},{1,17},{... | collective-permute-start | bytes 442376 | tf_op jit(solution)/shard_map/ppermute | solution.py:106
  (25 other events, 119.4 us)
where the time goes:
time: 188 us; the launch traced here: 187 us
  waiting for transfers between devices  64.9 us (35%)
  starting transfers between devices  41.7 us (22%)
  Pallas kernels  31.3 us (17%)
  local copies, waits for them, and re-layouts  29.7 us (16%)
  other arithmetic  12.2 us (6%)
  matrix products  6.11 us (3%)
    ppermute x30, waiting for transfers between devices, swap(): return lax.ppermute(x, axis, [(i, i ^ bit) for i in range(n)])  64.9 us
    ppermute x30, starting transfers between devices, swap(): return lax.ppermute(x, axis, [(i, i ^ bit) for i in range(n)])  41.7 us
    pallas_call x2, Pallas kernels, project(): pl.pallas_call(body, grid_spec=pltpu.PrefetchScalarGridSpec(num_scalar_pr...  31.3 us
    reshape x6, local copies, waits for them, and re-layouts, shards(): blocks[start:start + rows].reshape(count // per_group, side, side)  11.3 us
    add x12, other arithmetic, shards(): s = mine + swap(other, 'gc', bit)  5.15 us
    add x6, other arithmetic, shards(): sums.append(outs[2 * c] + swap(outs[2 * c + 1], 'gr', 1))  4.56 us
    dot_general x6, matrix products, shards(): lax.dot_general(blocks[start:start + rows].reshape(count // per_group, si...  3.95 us
  transfers between devices with their start and end apart: 30, of which 17 were waited for; matrix products, arithmetic and copies ran while one was open for 23% of the time, Pallas kernels for 11%

commit v1 on v0

--- a/solution.py
+++ b/solution.py
@@ -138,8 +138,6 @@
     sums, spans, offset = [], [], 0
     for sizes in PLAN:
         outs = list(project(columns, waves, atom_order, me, gc, nh, per_block, offset, sizes))
-        if offset > 0:
-            coupling, outs[-2] = lax.optimization_barrier((coupling, outs[-2]))
         for c, size in enumerate(sizes):
             spans.append((offset * per_block * nh, size * per_block))
             offset += size
@@ -147,26 +145,20 @@
         if offset < UNITS:
             me, sums[-1] = lax.optimization_barrier((me, sums[-1]))
 
-    per_group = min(8, per_block)
-    side = per_group * nh
-    at = jnp.arange(side, dtype=jnp.int32)
-    repeat = (jnp.arange(nh, dtype=jnp.int32)[:, None] == (at % nh)[None, :]).astype(jnp.float32)
-    wide = jnp.dot(coupling.reshape(local_atoms * nh, nh), repeat, precision=lax.Precision.HIGHEST)
-    atom_of = (jnp.arange(local_atoms * nh, dtype=jnp.int32) // nh) % per_group
-    blocks = jnp.where(atom_of[:, None] == (at // nh)[None, :], wide, 0.0)
-
-    pieces = []
+    reduced = []
     for c, (s, (start, count)) in enumerate(zip(sums, spans)):
         rows = count * nh
         bits = bits_of(gc)
         s = s.reshape([2] * len(bits) + [rows, s.shape[1]])
         left = bits[::-1]
-        for bit in bits if c % 2 == 0 else bits[::-1]:
+        for n, bit in enumerate(bits if c % 2 == 0 else bits[::-1]):
             axis = left.index(bit)
             left = left[:axis] + left[axis + 1:]
             mine = lax.index_in_dim(s, 0, axis, keepdims=False)
             other = lax.index_in_dim(s, 1, axis, keepdims=False)
             s = mine + swap(other, "gc", bit)
+            if c == 2 and n == 0:
+                coupling, s = lax.optimization_barrier((coupling, s))
         for bit in bits_of(nz):
             half = s.shape[1] // 2
             fold = max(1, LANES // half)
@@ -177,6 +169,19 @@
             if fold > 1:
                 got = jnp.concatenate(jnp.split(got, fold, axis=1), axis=0)
             s = s[:, :half] + got
+        reduced.append(s)
+
+    per_group = min(8, per_block)
+    side = per_group * nh
+    at = jnp.arange(side, dtype=jnp.int32)
+    repeat = (jnp.arange(nh, dtype=jnp.int32)[:, None] == (at % nh)[None, :]).astype(jnp.float32)
+    wide = jnp.dot(coupling.reshape(local_atoms * nh, nh), repeat, precision=lax.Precision.HIGHEST)
+    atom_of = (jnp.arange(local_atoms * nh, dtype=jnp.int32) // nh) % per_group
+    blocks = jnp.where(atom_of[:, None] == (at // nh)[None, :], wide, 0.0)
+
+    pieces = []
+    for s, (start, count) in zip(reduced, spans):
+        rows = count * nh
         done = lax.dot_general(
             blocks[start:start + rows].reshape(count // per_group, side, side),
             s.reshape(count // per_group, side, s.shape[1]), (((2,), (1,)), ((0,), (0,))),

time: 188 us -> 180 us (0.957)
  waiting for transfers between devices: 64.9 us -> 75.4 us
  local copies, waits for them, and re-layouts: 29.7 us -> 19.3 us
  starting transfers between devices: 41.7 us -> 35.3 us
  other arithmetic: 12.2 us -> 10 us
    ppermute x30, waiting for transfers between devices: 64.9 us -> 75.4 us  [swap(): return lax.ppermute(x, axis, [(i, i ^ bit) for i in range(n)])]
    reshape x6, local copies, waits for them, and re-layouts: 11.3 us -> 2.62 us  [shards(): blocks[start:start + rows].reshape(count // per_group, side, side)]
    ppermute x30, starting transfers between devices: 41.7 us -> 35.3 us  [swap(): return lax.ppermute(x, axis, [(i, i ^ bit) for i in range(n)])]
    add x6, other arithmetic: 4.56 us -> 1.23 us  [shards(): sums.append(outs[2 * c] + swap(outs[2 * c + 1], 'gr', 1))]
    dot_general x6, matrix products: 3.95 us -> 6.57 us  [shards(): lax.dot_general(blocks[start:start + rows].reshape(count // per_group, si...]
    reshape x6, local copies, waits for them, and re-layouts: 0.96 us -> 3.48 us  [shards(): pieces.append(done.reshape(rows, s.shape[1]))]
    add x12, other arithmetic: 1.27 us -> 3.26 us  [shards(): s = s[:, :half] + got]
    optimization_barrier x1, local copies, waits for them, and re-layouts: 2.38 us -> 0.4 us  [shards(): coupling, s = lax.optimization_barrier((coupling, s))]
  transfers between devices with their start and end apart: 30 -> 30, of which waited for: 17 -> 18; matrix products, arithmetic and copies ran while one was open for 23% -> 17% of each run, Pallas kernels for 11% -> 11%
where the time goes in v1:
time: 180 us
  waiting for transfers between devices  75.4 us (42%)
  starting transfers between devices  35.3 us (20%)
  Pallas kernels  31.3 us (17%)
  local copies, waits for them, and re-layouts  19.3 us (11%)
  other arithmetic  10 us (6%)
  matrix products  7.73 us (4%)
    ppermute x30, waiting for transfers between devices, swap(): return lax.ppermute(x, axis, [(i, i ^ bit) for i in range(n)])  75.4 us
    ppermute x30, starting transfers between devices, swap(): return lax.ppermute(x, axis, [(i, i ^ bit) for i in range(n)])  35.3 us
    pallas_call x2, Pallas kernels, project(): pl.pallas_call(body, grid_spec=pltpu.PrefetchScalarGridSpec(num_scalar_pr...  31.3 us
    dot_general x6, matrix products, shards(): lax.dot_general(blocks[start:start + rows].reshape(count // per_group, si...  6.57 us
    add x12, other arithmetic, shards(): s = mine + swap(other, 'gc', bit)  4.89 us
  transfers between devices with their start and end apart: 30, of which 18 were waited for; matrix products, arithmetic and copies ran while one was open for 17% of the time, Pallas kernels for 11%

profile of v1, /device:TPU:0, one launch (start us, length us, event | category | flops | bytes accessed | tf_op | source)
XLA Modules:
  0.0 179.8 jit_solution(16328249283579817017)
XLA Ops:
  1.5 11.1 %shard_map.46 = (f32[1152,256]{1,0:T(8,128)S(1)}, f32[1152,256]{1,0:T(8,128)S(1)}, f32[1152,256]{1,0:T(8,128)S(1)}, f32[1152,256]{1,0:T(8,128)S(1)}) custom-call(s32[512]{0:T(512)S(1)} %copy-done.2, s32[1]{0:T(128)} %bitcast.me_ref, bf16[512,9216]{1,0:T(8,128)(2,1)} %bitcast.142, bf16[512,512]{1,0:T(8,128)(2,1)S(1)} %fusion.waves_ref), custom_call_target="tpu_custom_call" | custom-call | flops 4831838208 | bytes 28311552 | tf_op jit(solution)/shard_map/pallas_call | solution.py:82
  13.2 2.4 %collective-permute-done = f32[1152,256]{1,0:T(8,128)S(1)} collective-permute-done((f32[1152,256]{1,0:T(8,128)S(1)}, f32[1152,256]{1,0:T(8,128)S(1)}, u32[]{:S(2)}, u32[]{:S(2)}) %collective-permute-start) | collective-permute-done | bytes 1179680 | tf_op jit(solution)/shard_map/ppermute | solution.py:106
  15.8 2.9 %collective-permute-start.8 = (f32[2,288,256]{2,1,0:T(8,128)S(1)}, f32[2,288,256]{2,1,0:T(8,128)S(1)}, u32[]{:S(2)}, u32[]{:S(2)}) collective-permute-start(f32[2,288,256]{2,1,0:T(8,128)S(1)} %bitcast.141), channel_id=1, source_target_pairs={{0,2},{1,3},{2,0},{3,1},{4,6},{5,7},{6,4},{7,5},{8,10},{9,11},{10,... | collective-permute-start | bytes 1769480 | tf_op jit(solution)/shard_map/ppermute | solution.py:106
  20.6 11.8 %collective-permute-done.8 = f32[2,288,256]{2,1,0:T(8,128)S(1)} collective-permute-done((f32[2,288,256]{2,1,0:T(8,128)S(1)}, f32[2,288,256]{2,1,0:T(8,128)S(1)}, u32[]{:S(2)}, u32[]{:S(2)}) %collective-permute-start.8) | collective-permute-done | bytes 589856 | tf_op jit(solution)/shard_map/ppermute | solution.py:106
  32.5 1.8 collective-permute-start.9
  36.0 20.2 %shard_map.47 = (f32[2304,256]{1,0:T(8,128)}, f32[2304,256]{1,0:T(8,128)}, f32[2304,256]{1,0:T(8,128)}, f32[2304,256]{1,0:T(8,128)}, f32[1152,256]{1,0:T(8,128)S...) custom-call(s32[512]{0:T(512)S(1)} %copy-done.2, s32[1]{0:T(128)} %bitcast.me_ref, ...), custom_call_target="tpu_custom_call" | custom-call | flops 4831838208 | bytes 28311552 | tf_op jit(solution)/shard_map/pallas_call | solution.py:82
  59.0 4.2 %collective-permute-done.10 = f32[288,128]{1,0:T(8,128)S(1)} collective-permute-done((f32[288,128]{1,0:T(8,128)S(1)}, f32[288,128]{1,0:T(8,128)S(1)}, u32[]{:S(2)}, u32[]{:S(2)}) %collective-permute-start.10) | collective-permute-done | bytes 147488 | tf_op jit(solution)/shard_map/ppermute | solution.py:106
  65.0 3.3 %collective-permute-done.6 = f32[288,128]{1,0:T(8,128)S(1)} collective-permute-done((f32[288,128]{1,0:T(8,128)S(1)}, f32[288,128]{1,0:T(8,128)S(1)}, u32[]{:S(2)}, u32[]{:S(2)}) %collective-permute-start.6) | collective-permute-done | bytes 147488 | tf_op jit(solution)/shard_map/ppermute | solution.py:106
  68.3 2.6 %collective-permute-start.11 = (f32[144,128]{1,0:T(8,128)S(1)}, f32[144,128]{1,0:T(8,128)S(1)}, u32[]{:S(2)}, u32[]{:S(2)}) collective-permute-start(f32[144,128]{1,0:T(8,128)S(1)} %pad_maximum_fusion.3), channel_id=1, source_target_pairs={{0,16},{4,20},{8,24},{12,28},{16,0},{20,4},{24,8},{28,12},{1,17},{... | collective-permute-start | bytes 221192 | tf_op jit(solution)/shard_map/ppermute | solution.py:106
  71.1 2.4 %collective-permute-done.11 = f32[144,128]{1,0:T(8,128)S(1)} collective-permute-done((f32[144,128]{1,0:T(8,128)S(1)}, f32[144,128]{1,0:T(8,128)S(1)}, u32[]{:S(2)}, u32[]{:S(2)}) %collective-permute-start.11) | collective-permute-done | bytes 73760 | tf_op jit(solution)/shard_map/ppermute | solution.py:106
  73.6 2.7 %collective-permute-start.7 = (f32[144,128]{1,0:T(8,128)S(1)}, f32[144,128]{1,0:T(8,128)S(1)}, u32[]{:S(2)}, u32[]{:S(2)}) collective-permute-start(f32[144,128]{1,0:T(8,128)S(1)} %pad_maximum_fusion.2), channel_id=1, source_target_pairs={{0,16},{4,20},{8,24},{12,28},{16,0},{20,4},{24,8},{28,12},{1,17},{... | collective-permute-start | bytes 221192 | tf_op jit(solution)/shard_map/ppermute | solution.py:106
  79.0 9.7 %collective-permute-done.21 = f32[2,288,256]{2,1,0:T(8,128)S(1)} collective-permute-done((f32[2,288,256]{2,1,0:T(8,128)S(1)}, f32[2,288,256]{2,1,0:T(8,128)S(1)}, u32[]{:S(2)}, u32[]{:S(2)}) %collective-permute-start.21) | collective-permute-done | bytes 589856 | tf_op jit(solution)/shard_map/ppermute | solution.py:106
  89.2 3.8 %collective-permute-done.26 = f32[2,288,256]{2,1,0:T(8,128)S(1)} collective-permute-done((f32[2,288,256]{2,1,0:T(8,128)S(1)}, f32[2,288,256]{2,1,0:T(8,128)S(1)}, u32[]{:S(2)}, u32[]{:S(2)}) %collective-permute-start.26) | collective-permute-done | bytes 589856 | tf_op jit(solution)/shard_map/ppermute | solution.py:106
  93.9 2.4 %collective-permute-done.22 = f32[288,256]{1,0:T(8,128)S(1)} collective-permute-done((f32[288,256]{1,0:T(8,128)S(1)}, f32[288,256]{1,0:T(8,128)S(1)}, u32[]{:S(2)}, u32[]{:S(2)}) %collective-permute-start.22) | collective-permute-done | bytes 294944 | tf_op jit(solution)/shard_map/ppermute | solution.py:106
  96.3 2.6 %collective-permute-start.23 = (f32[288,128]{1,0:T(8,128)S(1)}, f32[288,128]{1,0:T(8,128)S(1)}, u32[]{:S(2)}, u32[]{:S(2)}) collective-permute-start(f32[288,128]{1,0:T(8,128)S(1)} %slice.250), channel_id=1, source_target_pairs={{0,8},{4,12},{8,0},{12,4},{16,24},{20,28},{24,16},{28,20},{1,9},{5... | collective-permute-start | bytes 442376 | tf_op jit(solution)/shard_map/ppermute | solution.py:106
  100.0 2.4 %collective-permute-start.28 = (f32[288,128]{1,0:T(8,128)S(1)}, f32[288,128]{1,0:T(8,128)S(1)}, u32[]{:S(2)}, u32[]{:S(2)}) collective-permute-start(f32[288,128]{1,0:T(8,128)S(1)} %slice.258), channel_id=1, source_target_pairs={{0,8},{4,12},{8,0},{12,4},{16,24},{20,28},{24,16},{28,20},{1,9},{5... | collective-permute-start | bytes 442376 | tf_op jit(solution)/shard_map/ppermute | solution.py:106
  103.0 2.6 %collective-permute-done.28 = f32[288,128]{1,0:T(8,128)S(1)} collective-permute-done((f32[288,128]{1,0:T(8,128)S(1)}, f32[288,128]{1,0:T(8,128)S(1)}, u32[]{:S(2)}, u32[]{:S(2)}) %collective-permute-start.28) | collective-permute-done | bytes 147488 | tf_op jit(solution)/shard_map/ppermute | solution.py:106
  108.8 3.7 %collective-permute-start.2 = (f32[2,576,256]{2,1,0:T(8,128)S(1)}, f32[2,576,256]{2,1,0:T(8,128)S(1)}, u32[]{:S(2)}, u32[]{:S(2)}) collective-permute-start(f32[2,576,256]{2,1,0:T(8,128)S(1)} %slice_bitcast_fusion), channel_id=1, source_target_pairs={{0,1},{1,0},{2,3},{3,2},{4,5},{5,4},{6,7},{7,6},{8,9},{9,8},{10,11... | collective-permute-start | bytes 3538952 | tf_op jit(solution)/shard_map/ppermute | solution.py:106
  116.2 15.2 %collective-permute-done.2 = f32[2,576,256]{2,1,0:T(8,128)S(1)} collective-permute-done((f32[2,576,256]{2,1,0:T(8,128)S(1)}, f32[2,576,256]{2,1,0:T(8,128)S(1)}, u32[]{:S(2)}, u32[]{:S(2)}) %collective-permute-start.2) | collective-permute-done | bytes 1179680 | tf_op jit(solution)/shard_map/ppermute | solution.py:106
  136.9 4.5 %collective-permute-done.16 = f32[2,576,256]{2,1,0:T(8,128)} collective-permute-done((f32[2,576,256]{2,1,0:T(8,128)}, f32[2,576,256]{2,1,0:T(8,128)}, u32[]{:S(2)}, u32[]{:S(2)}) %collective-permute-start.16) | collective-permute-done | bytes 1179680 | tf_op jit(solution)/shard_map/ppermute | solution.py:106
  141.4 1.8 add.217
  153.7 1.8 collective-permute-start.13
  165.4 5.0 %collective-permute-done.18 = f32[576,128]{1,0:T(8,128)S(1)} collective-permute-done((f32[576,128]{1,0:T(8,128)S(1)}, f32[576,128]{1,0:T(8,128)S(1)}, u32[]{:S(2)}, u32[]{:S(2)}) %collective-permute-start.18) | collective-permute-done | bytes 294944 | tf_op jit(solution)/shard_map/ppermute | solution.py:106
  174.0 3.2 %collective-permute-done.19 = f32[288,128]{1,0:T(8,128)S(1)} collective-permute-done((f32[288,128]{1,0:T(8,128)S(1)}, f32[288,128]{1,0:T(8,128)S(1)}, u32[]{:S(2)}, u32[]{:S(2)}) %collective-permute-start.19) | collective-permute-done | bytes 147488 | tf_op jit(solution)/shard_map/ppermute | solution.py:106
  (174 shorter events, 55.0 us)
Async XLA Ops:
  15.8 16.6 %collective-permute-start.8 = (f32[2,288,256]{2,1,0:T(8,128)S(1)}, f32[2,288,256]{2,1,0:T(8,128)S(1)}, u32[]{:S(2)}, u32[]{:S(2)}) collective-permute-start(f32[2,288,256]{2,1,0:T(8,128)S(1)} %bitcast.141), channel_id=1, source_target_pairs={{0,2},{1,3},{2,0},{3,1},{4,6},{5,7},{6,4},{7,5},{8,10},{9,11},{10,... | collective-permute-start | bytes 1769480 | tf_op jit(solution)/shard_map/ppermute | solution.py:106
  19.0 15.3 %collective-permute-start.4 = (f32[2,288,256]{2,1,0:T(8,128)S(1)}, f32[2,288,256]{2,1,0:T(8,128)S(1)}, u32[]{:S(2)}, u32[]{:S(2)}) collective-permute-start(f32[2,288,256]{2,1,0:T(8,128)S(1)} %slice_bitcast_fusion.6), channel_id=1, source_target_pairs={{0,1},{1,0},{2,3},{3,2},{4,5},{5,4},{6,7},{7,6},{8,9},{9,8},{10,11... | collective-permute-start | bytes 1769480 | tf_op jit(solution)/shard_map/ppermute | solution.py:106
  32.5 24.3 %collective-permute-start.9 = (f32[288,256]{1,0:T(8,128)S(1)}, f32[288,256]{1,0:T(8,128)S(1)}, u32[]{:S(2)}, u32[]{:S(2)}) collective-permute-start(f32[288,256]{1,0:T(8,128)S(1)} %slice_bitcast_fusion.13), channel_id=1, source_target_pairs={{0,1},{1,0},{2,3},{3,2},{4,5},{5,4},{6,7},{7,6},{8,9},{9,8},{10,11... | collective-permute-start | bytes 884744 | tf_op jit(solution)/shard_map/ppermute | solution.py:106
  34.4 22.9 %collective-permute-start.5 = (f32[288,256]{1,0:T(8,128)S(1)}, f32[288,256]{1,0:T(8,128)S(1)}, u32[]{:S(2)}, u32[]{:S(2)}) collective-permute-start(f32[288,256]{1,0:T(8,128)S(1)} %slice_bitcast_fusion.15), channel_id=1, source_target_pairs={{0,2},{1,3},{2,0},{3,1},{4,6},{5,7},{6,4},{7,5},{8,10},{9,11},{10,... | collective-permute-start | bytes 884744 | tf_op jit(solution)/shard_map/ppermute | solution.py:106
  56.2 20.1 %collective-permute-start.20 = (f32[1152,256]{1,0:T(8,128)S(1)}, f32[1152,256]{1,0:T(8,128)S(1)}, u32[]{:S(2)}, u32[]{:S(2)}) collective-permute-start(f32[1152,256]{1,0:T(8,128)S(1)} %get-tuple-element.34), channel_id=1, source_target_pairs={{0,4},{4,0},{8,12},{12,8},{16,20},{20,16},{24,28},{28,24},{1,5},{5... | collective-permute-start | bytes 3538952 | tf_op jit(solution)/shard_map/ppermute | solution.py:106
  56.2 21.9 %collective-permute-start.25 = (f32[1152,256]{1,0:T(8,128)S(1)}, f32[1152,256]{1,0:T(8,128)S(1)}, u32[]{:S(2)}, u32[]{:S(2)}) collective-permute-start(f32[1152,256]{1,0:T(8,128)S(1)} %get-tuple-element.36), channel_id=1, source_target_pairs={{0,4},{4,0},{8,12},{12,8},{16,20},{20,16},{24,28},{28,24},{1,5},{5... | collective-permute-start | bytes 3538952 | tf_op jit(solution)/shard_map/ppermute | solution.py:106
  56.7 51.6 %collective-permute-start.1 = (f32[2304,256]{1,0:T(8,128)}, f32[2304,256]{1,0:T(8,128)S(1)}, u32[]{:S(2)}, u32[]{:S(2)}) collective-permute-start(f32[2304,256]{1,0:T(8,128)} %get-tuple-element.25), channel_id=1, source_target_pairs={{0,4},{4,0},{8,12},{12,8},{16,20},{20,16},{24,28},{28,24},{1,5},{5... | collective-permute-start | bytes 7077896 | tf_op jit(solution)/shard_map/ppermute | solution.py:106
  56.8 56.4 %collective-permute-start.15 = (f32[2304,256]{1,0:T(8,128)}, f32[2304,256]{1,0:T(8,128)S(1)}, u32[]{:S(2)}, u32[]{:S(2)}) collective-permute-start(f32[2304,256]{1,0:T(8,128)} %get-tuple-element.32), channel_id=1, source_target_pairs={{0,4},{4,0},{8,12},{12,8},{16,20},{20,16},{24,28},{28,24},{1,5},{5... | collective-permute-start | bytes 7077896 | tf_op jit(solution)/shard_map/ppermute | solution.py:106
  57.3 5.9 %collective-permute-start.10 = (f32[288,128]{1,0:T(8,128)S(1)}, f32[288,128]{1,0:T(8,128)S(1)}, u32[]{:S(2)}, u32[]{:S(2)}) collective-permute-start(f32[288,128]{1,0:T(8,128)S(1)} %slice.230), channel_id=1, source_target_pairs={{0,8},{4,12},{8,0},{12,4},{16,24},{20,28},{24,16},{28,20},{1,9},{5... | collective-permute-start | bytes 442376 | tf_op jit(solution)/shard_map/ppermute | solution.py:106
  76.5 12.1 %collective-permute-start.21 = (f32[2,288,256]{2,1,0:T(8,128)S(1)}, f32[2,288,256]{2,1,0:T(8,128)S(1)}, u32[]{:S(2)}, u32[]{:S(2)}) collective-permute-start(f32[2,288,256]{2,1,0:T(8,128)S(1)} %slice_bitcast_fusion.2), channel_id=1, source_target_pairs={{0,1},{1,0},{2,3},{3,2},{4,5},{5,4},{6,7},{7,6},{8,9},{9,8},{10,11... | collective-permute-start | bytes 1769480 | tf_op jit(solution)/shard_map/ppermute | solution.py:106
  78.3 14.6 %collective-permute-start.26 = (f32[2,288,256]{2,1,0:T(8,128)S(1)}, f32[2,288,256]{2,1,0:T(8,128)S(1)}, u32[]{:S(2)}, u32[]{:S(2)}) collective-permute-start(f32[2,288,256]{2,1,0:T(8,128)S(1)} %bitcast.140), channel_id=1, source_target_pairs={{0,2},{1,3},{2,0},{3,1},{4,6},{5,7},{6,4},{7,5},{8,10},{9,11},{10,... | collective-permute-start | bytes 1769480 | tf_op jit(solution)/shard_map/ppermute | solution.py:106
  88.8 7.5 %collective-permute-start.22 = (f32[288,256]{1,0:T(8,128)S(1)}, f32[288,256]{1,0:T(8,128)S(1)}, u32[]{:S(2)}, u32[]{:S(2)}) collective-permute-start(f32[288,256]{1,0:T(8,128)S(1)} %slice_bitcast_fusion.11), channel_id=1, source_target_pairs={{0,2},{1,3},{2,0},{3,1},{4,6},{5,7},{6,4},{7,5},{8,10},{9,11},{10,... | collective-permute-start | bytes 884744 | tf_op jit(solution)/shard_map/ppermute | solution.py:106
  93.1 6.8 %collective-permute-start.27 = (f32[288,256]{1,0:T(8,128)S(1)}, f32[288,256]{1,0:T(8,128)S(1)}, u32[]{:S(2)}, u32[]{:S(2)}) collective-permute-start(f32[288,256]{1,0:T(8,128)S(1)} %slice_bitcast_fusion.9), channel_id=1, source_target_pairs={{0,1},{1,0},{2,3},{3,2},{4,5},{5,4},{6,7},{7,6},{8,9},{9,8},{10,11... | collective-permute-start | bytes 884744 | tf_op jit(solution)/shard_map/ppermute | solution.py:106
  96.3 6.4 %collective-permute-start.23 = (f32[288,128]{1,0:T(8,128)S(1)}, f32[288,128]{1,0:T(8,128)S(1)}, u32[]{:S(2)}, u32[]{:S(2)}) collective-permute-start(f32[288,128]{1,0:T(8,128)S(1)} %slice.250), channel_id=1, source_target_pairs={{0,8},{4,12},{8,0},{12,4},{16,24},{20,28},{24,16},{28,20},{1,9},{5... | collective-permute-start | bytes 442376 | tf_op jit(solution)/shard_map/ppermute | solution.py:106
  100.0 5.7 %collective-permute-start.28 = (f32[288,128]{1,0:T(8,128)S(1)}, f32[288,128]{1,0:T(8,128)S(1)}, u32[]{:S(2)}, u32[]{:S(2)}) collective-permute-start(f32[288,128]{1,0:T(8,128)S(1)} %slice.258), channel_id=1, source_target_pairs={{0,8},{4,12},{8,0},{12,4},{16,24},{20,28},{24,16},{28,20},{1,9},{5... | collective-permute-start | bytes 442376 | tf_op jit(solution)/shard_map/ppermute | solution.py:106
  105.9 6.6 %collective-permute-start.29 = (f32[144,128]{1,0:T(8,128)S(1)}, f32[144,128]{1,0:T(8,128)S(1)}, u32[]{:S(2)}, u32[]{:S(2)}) collective-permute-start(f32[144,128]{1,0:T(8,128)S(1)} %pad_maximum_fusion.5), channel_id=1, source_target_pairs={{0,16},{4,20},{8,24},{12,28},{16,0},{20,4},{24,8},{28,12},{1,17},{... | collective-permute-start | bytes 221192 | tf_op jit(solution)/shard_map/ppermute | solution.py:106
  108.8 22.7 %collective-permute-start.2 = (f32[2,576,256]{2,1,0:T(8,128)S(1)}, f32[2,576,256]{2,1,0:T(8,128)S(1)}, u32[]{:S(2)}, u32[]{:S(2)}) collective-permute-start(f32[2,576,256]{2,1,0:T(8,128)S(1)} %slice_bitcast_fusion), channel_id=1, source_target_pairs={{0,1},{1,0},{2,3},{3,2},{4,5},{5,4},{6,7},{7,6},{8,9},{9,8},{10,11... | collective-permute-start | bytes 3538952 | tf_op jit(solution)/shard_map/ppermute | solution.py:106
  115.0 26.3 %collective-permute-start.16 = (f32[2,576,256]{2,1,0:T(8,128)}, f32[2,576,256]{2,1,0:T(8,128)}, u32[]{:S(2)}, u32[]{:S(2)}) collective-permute-start(f32[2,576,256]{2,1,0:T(8,128)} %bitcast.26), channel_id=1, source_target_pairs={{0,2},{1,3},{2,0},{3,1},{4,6},{5,7},{6,4},{7,5},{8,10},{9,11},{10,... | collective-permute-start | bytes 3538952 | tf_op jit(solution)/shard_map/ppermute | solution.py:106
  133.5 18.1 %collective-permute-start.12 = (f32[576,256]{1,0:T(8,128)}, f32[576,256]{1,0:T(8,128)}, u32[]{:S(2)}, u32[]{:S(2)}) collective-permute-start(f32[576,256]{1,0:T(8,128)} %slice_bitcast_fusion.8), channel_id=1, source_target_pairs={{0,2},{1,3},{2,0},{3,1},{4,6},{5,7},{6,4},{7,5},{8,10},{9,11},{10,... | collective-permute-start | bytes 1769480 | tf_op jit(solution)/shard_map/ppermute | solution.py:106
  144.1 17.5 %collective-permute-start.17 = (f32[576,256]{1,0:T(8,128)}, f32[576,256]{1,0:T(8,128)}, u32[]{:S(2)}, u32[]{:S(2)}) collective-permute-start(f32[576,256]{1,0:T(8,128)} %slice_bitcast_fusion.4), channel_id=1, source_target_pairs={{0,1},{1,0},{2,3},{3,2},{4,5},{5,4},{6,7},{7,6},{8,9},{9,8},{10,11... | collective-permute-start | bytes 1769480 | tf_op jit(solution)/shard_map/ppermute | solution.py:106
  153.7 9.9 %collective-permute-start.13 = (f32[576,128]{1,0:T(8,128)}, f32[576,128]{1,0:T(8,128)}, u32[]{:S(2)}, u32[]{:S(2)}) collective-permute-start(f32[576,128]{1,0:T(8,128)} %slice.234), channel_id=1, source_target_pairs={{0,8},{4,12},{8,0},{12,4},{16,24},{20,28},{24,16},{28,20},{1,9},{5... | collective-permute-start | bytes 884744 | tf_op jit(solution)/shard_map/ppermute | solution.py:106
  162.8 7.6 %collective-permute-start.18 = (f32[576,128]{1,0:T(8,128)S(1)}, f32[576,128]{1,0:T(8,128)S(1)}, u32[]{:S(2)}, u32[]{:S(2)}) collective-permute-start(f32[576,128]{1,0:T(8,128)S(1)} %slice.242), channel_id=1, source_target_pairs={{0,8},{4,12},{8,0},{12,4},{16,24},{20,28},{24,16},{28,20},{1,9},{5... | collective-permute-start | bytes 884744 | tf_op jit(solution)/shard_map/ppermute | solution.py:106
  164.9 7.7 %collective-permute-start.14 = (f32[288,128]{1,0:T(8,128)S(1)}, f32[288,128]{1,0:T(8,128)S(1)}, u32[]{:S(2)}, u32[]{:S(2)}) collective-permute-start(f32[288,128]{1,0:T(8,128)S(1)} %pad_maximum_fusion), channel_id=1, source_target_pairs={{0,16},{4,20},{8,24},{12,28},{16,0},{20,4},{24,8},{28,12},{1,17},{... | collective-permute-start | bytes 442376 | tf_op jit(solution)/shard_map/ppermute | solution.py:106
  170.7 6.5 %collective-permute-start.19 = (f32[288,128]{1,0:T(8,128)S(1)}, f32[288,128]{1,0:T(8,128)S(1)}, u32[]{:S(2)}, u32[]{:S(2)}) collective-permute-start(f32[288,128]{1,0:T(8,128)S(1)} %pad_maximum_fusion.1), channel_id=1, source_target_pairs={{0,16},{4,20},{8,24},{12,28},{16,0},{20,4},{24,8},{28,12},{1,17},{... | collective-permute-start | bytes 442376 | tf_op jit(solution)/shard_map/ppermute | solution.py:106
  (24 other events, 78.3 us)
